TPU v7x, 256 devices: a 4x2x16 block of a 4x16x16 slice. The times are simulated.
256 devices in a mesh: group: 2 (over y), pool: 2 (over core), slab: 64 (over z, x).
Axes of the slice: x: 4, y: 2, z: 16, core: 2. Of those that a mesh axis runs over, the one named last changes fastest.
The devices are a block of a 4x16x16 slice.
Arguments:
- drho_part: float32 [2, 32, 2, 128, 128, 128], P('pool', 'group', None, 'slab'), parts along dimension 1, may hold values from -6 to 6
- fxc: float32 [128, 128, 128], P('slab'), may hold values from -2 to -0.2
- cutoff_mask: int32 [128, 128, 128], P(None, 'slab'), may hold values 0 or 1
- owner_table: int32 [32], P('group'), parts along dimension 0, may hold values from 0 to 15, each once
Outputs:
- dv: float32 [32, 2, 128, 128, 128], P('group', None, 'slab'), parts along dimension 0
There are 2 independent parts, one for each index of `group`. A program takes and returns all parts, laid end to end along the dimension named above; an argument that names none is the same for every part. Nothing has to cross between parts.
Inputs may be any that keep to these rules, and one draw needn't show every extreme that they name: `owner_table`: each perturbation appears in exactly one slot.
All inputs are finite; a program needn't handle non-finite values. No bound on the sum of `cutoff_mask` on one device may be relied on, other than what follows from the above.
Results may differ from a plain program's by a relative error of at most 0.00008.
Values sent between devices are 32-bit elements; how exact they have to be, the bound alone decides.
A program may use at most 64 MiB of HBM per device.

v0:
```python
import math

import jax
import jax.numpy as jnp
from jax import lax
from jax.sharding import PartitionSpec as P


def split_up(value, dim, length):
    before, after = (value.shape[:dim], value.shape[dim + 1 :])
    return jnp.moveaxis(value.reshape(*before, length, -1, *after), dim, 0)


def sent_and_summed(value, axis, dim):
    pieces = split_up(value, dim, lax.axis_size(axis))
    arrived = lax.all_to_all(pieces, axis, split_axis=0, concat_axis=0, tiled=True)
    return arrived.sum(axis=0)


def dft_tables(length):
    index = jnp.arange(length, dtype=jnp.int32)
    phase = index[:, None] * index[None, :] % length
    angle = phase.astype(jnp.float32) * (2.0 * math.pi / length)
    return (jnp.cos(angle), jnp.sin(angle))


def transform(field, form, cosine, sine, orient):
    real_part = field[:, 0]
    imag_part = field[:, 1]
    highest = lax.Precision.HIGHEST
    real_cos = jnp.einsum(form, real_part, cosine, precision=highest)
    real_sin = jnp.einsum(form, real_part, sine, precision=highest)
    imag_cos = jnp.einsum(form, imag_part, cosine, precision=highest)
    imag_sin = jnp.einsum(form, imag_part, sine, precision=highest)
    return jnp.stack([real_cos - orient * imag_sin, imag_cos + orient * real_sin], axis=1)


def frequency(index, length):
    return ((index + length // 2) % length - length // 2).astype(jnp.float32)


def column_kernel(cutoff_mask, length):
    width = cutoff_mask.shape[1]
    start = lax.axis_index("slab") * width
    full_index = jnp.arange(length, dtype=jnp.int32)
    part_index = start + jnp.arange(width, dtype=jnp.int32)
    full_square = frequency(full_index, length) ** 2
    part_square = frequency(part_index, length) ** 2
    total = full_square[:, None, None] + part_square[None, :, None] + full_square[None, None, :]
    unit = (2.0 * math.pi / length) ** 2
    return 4.0 * math.pi * cutoff_mask.astype(jnp.float32) / (unit * total + 0.25)


def potentials(density, fxc, cutoff_mask):
    length = density.shape[-1]
    cosine, sine = dft_tables(length)
    along_z = "abcd,de->abce"
    along_y = "abcd,ce->abed"
    along_x = "abcd,be->aecd"
    spectrum = transform(density, along_z, cosine, sine, -1.0)
    spectrum = transform(spectrum, along_y, cosine, sine, -1.0)
    kernel = column_kernel(cutoff_mask, length)
    columns = lax.all_to_all(spectrum, "slab", split_axis=3, concat_axis=2, tiled=True)
    columns = transform(columns, along_x, cosine, sine, -1.0)
    columns = columns * kernel[None, None]
    columns = transform(columns, along_x, cosine, sine, 1.0)
    result = lax.all_to_all(columns, "slab", split_axis=2, concat_axis=3, tiled=True)
    result = transform(result, along_y, cosine, sine, 1.0)
    result = transform(result, along_z, cosine, sine, 1.0)
    scale = 1.0 / float(length * length * length)
    return result * scale + fxc[None, None] * density


def per_device(drho_part, fxc, cutoff_mask, owner_table):
    local = drho_part[0]
    ordered = jnp.take(local, owner_table, axis=0)
    owned = sent_and_summed(ordered, "pool", 0)
    result = potentials(owned, fxc, cutoff_mask)
    return lax.all_gather(result, "pool", axis=0, tiled=True)


def solution(mesh):
    placed = (
        P("pool", "group", None, "slab", None, None),
        P("slab", None, None),
        P(None, "slab", None),
        P("group"),
    )
    return jax.shard_map(
        per_device,
        mesh=mesh,
        in_specs=placed,
        out_specs=P("group", None, "slab", None, None),
        check_vma=False,
    )
```

profile of v0, /device:TPU:33, one launch (start us, length us, event | category | flops | bytes accessed | tf_op | source)
XLA Modules:
  0.0 341.3 jit_solution(2144675472239945557)
XLA Ops:
  6.5 0.7 compare_select_fusion
  7.2 0.7 compare_and_fusion
  7.9 0.1 broadcast_in_dim.21
  8.0 5.0 %gather_fusion = f32[16,2,2,128,128]{4,3,2,1,0:T(8,128)} fusion(f32[16,2,2,128,128]{4,3,2,1,0:T(8,128)} %bitcast.162, s32[1024]{0:T(1024)S(1)} %pad_clamp_fusion), kind=kCustom, calls=%fused_computation | custom fusion | bytes 8388672 | tf_op jit(solution)/shard_map/jit(_take)/gather | solution.py:76
  13.0 2.6 broadcast_select_fusion
  15.6 28.2 %all_to_all.41 = f32[2,8,2,2,128,128]{5,4,3,2,1,0:T(8,128)} all-to-all(f32[2,8,2,2,128,128]{5,4,3,2,1,0:T(8,128)S(1)} %broadcast_select_fusion), channel_id=1, replica_groups=mesh['group'=2,'pool'=2,'slab'=64] {'pool'}, dimensions={0} | all-to-all | bytes 8388608 | tf_op jit(solution)/shard_map/all_to_all | solution.py:16
  43.8 2.7 reduce_sum.9
  46.5 1.2 fusion.17
  47.7 1.2 fusion.18
  49.0 1.2 fusion.16
  50.2 1.3 fusion.51
  51.5 1.2 fusion.15
  52.7 1.3 fusion.43
  54.0 1.3 fusion.14
  55.4 1.3 fusion.12
  56.7 0.2 pad_maximum_fusion
  56.9 3.2 copy.31
  60.1 9.9 %all-to-all-start.1 = ((f32[8,2,2,128,128]{4,2,0,1,3:T(2,128)}), f32[8,2,2,128,128]{4,2,0,1,3:T(2,128)}, u32[]{:S(2)}, u32[]{:S(2)}) async-start(f32[8,2,2,128,128]{4,2,0,1,3:T(2,128)} %copy.31), calls=%async_computation.1 | async-start | bytes 4194304 | tf_op jit(solution)/shard_map/all_to_all | solution.py:63
  70.1 0.1 all-gather.2.cloned.1.call-start
  70.2 0.1 broadcast_add_fusion
  70.3 0.2 add_divide_fusion
  70.5 94.8 %all-to-all-done.1 = f32[8,2,2,128,128]{4,2,0,1,3:T(2,128)} async-done(((f32[8,2,2,128,128]{4,2,0,1,3:T(2,128)}), f32[8,2,2,128,128]{4,2,0,1,3:T(2,128)}, u32[]{:S(2)}, u32[]{:S(2)}) %all-to-all-start.1) | async-done | bytes 2097184 | tf_op jit(solution)/shard_map/all_to_all | solution.py:63
  165.3 2.7 copy.32
  168.0 1.3 fusion.19
  169.3 1.3 fusion.20
  170.6 1.3 fusion.10
  172.0 1.3 fusion.8
  173.3 0.2 maximum_multiply_fusion
  173.5 1.3 fusion.21
  174.8 1.3 fusion.22
  176.1 1.3 fusion.6
  177.4 1.3 fusion.5
  178.8 0.2 pad_maximum_fusion.1
  179.0 11.8 %copy.42 = f32[8,2,128,2,128]{4,3,0,1,2:T(2,128)S(1)} copy(f32[8,2,128,2,128]{4,2,3,0,1:T(8,128)S(1)} %pad_maximum_fusion.1) | data formatting | bytes 4194304 | tf_op jit(solution)/shard_map/stack | solution.py:35
  190.8 103.6 %all_to_all.42 = f32[8,2,128,2,128]{4,3,0,1,2:T(2,128)S(1)} all-to-all(f32[8,2,128,2,128]{4,3,0,1,2:T(2,128)S(1)} %copy.42), channel_id=1, replica_groups=mesh['group'=2,'pool'=2,'slab'=64] {'slab'}, dimensions={2} | all-to-all | bytes 4194304 | tf_op jit(solution)/shard_map/all_to_all | solution.py:67
  294.4 1.1 copy.43
  295.5 1.3 fusion.23
  296.8 1.3 fusion.24
  298.1 1.3 fusion.4
  299.4 1.2 fusion.47
  300.6 1.3 fusion.3
  301.9 1.2 fusion.45
  303.1 1.2 fusion.2
  304.4 1.2 fusion.1
  305.6 1.7 fusion
  307.4 0.1 all-gather.2.cloned.1.call-update
  307.4 22.1 %all-gather.2.cloned.1.call-done = f32[16,2,2,128,128]{4,3,2,0,1:T(8,128)} async-done(((f32[8,2,2,128,128]{4,3,2,0,1:T(8,128)}), f32[16,2,2,128,128]{4,3,2,0,1:T(8,128)}) %all-gather.2.cloned.1.call-update) | async-done | bytes 4194320 | tf_op jit(solution)/shard_map/all_gather | solution.py:79
  329.5 4.7 %copy.49 = f32[16,2,2,128,128]{4,3,2,1,0:T(8,128)} copy(f32[16,2,2,128,128]{4,3,2,0,1:T(8,128)} %all-gather.2.cloned.1.call-done) | data formatting | bytes 8388608 | tf_op jit(solution)/shard_map/all_gather | solution.py:79
  (8 shorter events, 0.1 us)
Async XLA Ops:
  60.1 10.1 %copy-start = (s32[128,2,128]{2,1,0:T(2,128)S(1)}, s32[128,2,128]{2,1,0:T(2,128)}, u32[]{:S(2)}) copy-start(s32[128,2,128]{2,1,0:T(2,128)} %param.6) | copy-start | bytes 393220
  60.1 105.2 %all-to-all-start.1 = ((f32[8,2,2,128,128]{4,2,0,1,3:T(2,128)}), f32[8,2,2,128,128]{4,2,0,1,3:T(2,128)}, u32[]{:S(2)}, u32[]{:S(2)}) async-start(f32[8,2,2,128,128]{4,2,0,1,3:T(2,128)} %copy.31), calls=%async_computation.1 | async-start | bytes 4194304 | tf_op jit(solution)/shard_map/all_to_all | solution.py:63
  70.1 259.4 %all-gather.2.cloned.1.call-start = ((), (), s32[]{:S(2)}) async-start(), calls=%async_computation.3 | async-start | bytes 6291456 | tf_op jit(solution)/shard_map/all_gather | solution.py:79
  304.4 1.3 copy-start.1
Sparse Core Ops, SparseCore 0:
  307.5 21.9 all-gather.1
where the time goes:
time: 346 us; the launch traced here: 341 us
  blocking collectives  132 us (38%)
  waiting for transfers between devices  117 us (34%)
  matrix products  30.6 us (9%)
  local copies, waits for them, and re-layouts  28.6 us (8%)
  between operations  13.9 us (4%)
  starting transfers between devices  9.98 us (3%)
  other arithmetic  9.35 us (3%)
    all_to_all x1, blocking collectives, potentials(): lax.all_to_all(columns, 'slab', split_axis=2, concat_axis=3, tiled=True)  104 us
    all_to_all x1, waiting for transfers between devices, potentials(): lax.all_to_all(spectrum, 'slab', split_axis=3, concat_axis=2, tiled=True)  94.8 us
    all_to_all x1, blocking collectives, sent_and_summed(): lax.all_to_all(pieces, axis, split_axis=0, concat_axis=0, tiled=True)  28.2 us
    all_gather x1, waiting for transfers between devices, per_device(): return lax.all_gather(result, 'pool', axis=0, tiled=True)  22.1 us
    another operation x2, local copies, waits for them, and re-layouts, transform(): jnp.stack([real_cos - orient * imag_sin, imag_cos + orient * real_sin], a...  15 us
    all_to_all x1, starting transfers between devices, potentials(): lax.all_to_all(spectrum, 'slab', split_axis=3, concat_axis=2, tiled=True)  9.92 us
    dot_general x6, matrix products, transform(): imag_sin = jnp.einsum(form, imag_part, sine, precision=highest)  7.72 us
    dot_general x6, matrix products, transform(): real_sin = jnp.einsum(form, real_part, sine, precision=highest)  7.71 us
  transfers between devices with their start and end apart: 2, of which 2 were waited for; matrix products, arithmetic and copies ran while one was open for 0% of the time, Pallas kernels for 0%

commit v1 on v0

v1 whole, which is shorter than its diff:
```python
import functools
import math

import jax
import jax.numpy as jnp
import numpy as np
from jax import lax
from jax.experimental import pallas as pl
from jax.experimental.pallas import tpu as pltpu
from jax.sharding import PartitionSpec as P

MESH = pl.DeviceIdType.MESH


def complex_form(table):
    return np.block([[table.real, -table.imag], [table.imag, table.real]])


def two_halves(table):
    high = table.astype(np.float32).astype(jnp.bfloat16)
    low = (table - high.astype(np.float64)).astype(np.float32).astype(jnp.bfloat16)
    return np.stack([high, low])


def dft_tables(length, width):
    tiles = length // width
    index = np.arange(length)
    phase = np.exp(-2j * math.pi * (index[:, None] * index[None, :] % length) / length)
    lanes = complex_form(phase).T
    real = complex_form(phase).reshape(2, length, 2, length)
    same = np.eye(width)
    cut = real.reshape(2, tiles, width, 2, length)
    spread = np.einsum("atibn,mk->tamibkn", cut, same)
    spread = spread.reshape(tiles * 2 * width * width, 2 * width * length)
    cut = real.reshape(2, length, 2, tiles, width)
    gather = np.einsum("anbtm,ik->aintbmk", cut, same)
    gather = gather.reshape(2 * width * length, tiles * 2 * width * width)
    return two_halves(lanes), two_halves(spread), two_halves(gather)


def split(value):
    high = value.astype(jnp.bfloat16)
    low = (value - high.astype(jnp.float32)).astype(jnp.bfloat16)
    return high, low


def from_left(table, value):
    high, low = split(value)
    lanes = value.shape[1]
    both = jnp.concatenate([high, low], axis=1)
    most = jnp.dot(table[0], both, preferred_element_type=jnp.float32)
    rest = jnp.dot(table[1], high, preferred_element_type=jnp.float32)
    return most[:, :lanes] + (most[:, lanes:] + rest)


def along_lanes(table, value):
    high, low = split(value)
    rows = value.shape[0]
    both = jnp.concatenate([high, low], axis=0)
    most = jnp.dot(both, table[0], preferred_element_type=jnp.float32)
    rest = jnp.dot(high, table[1], preferred_element_type=jnp.float32)
    return most[:rows] + (most[rows:] + rest)


def frequency(index, length):
    return ((index + length // 2) % length - length // 2).astype(jnp.float32)


def body(
    slabs, pools, owner_ref, drho_hbm, fxc_hbm, mask_hbm, lanes_hbm, spread_hbm, gather_hbm, out_hbm,
    drho, fxc, mask, lanes, spread, gather, kernel, other, given, density, sent, columns, back, final, result,
    load_sem, other_sem, send_sem, column_sem, final_sem, out_sem,
):
    me = lax.axis_index("slab")
    pool = lax.axis_index("pool")
    partner = pools - 1 - pool
    owned = given.shape[0]
    rows, length = given.shape[1:]
    half = rows // 2
    width = mask.shape[1]

    loads = [
        pltpu.make_async_copy(source, target, load_sem.at[n])
        for n, (source, target) in enumerate(
            [
                (drho_hbm, drho),
                (lanes_hbm, lanes),
                (spread_hbm, spread),
                (gather_hbm, gather),
                (mask_hbm, mask),
                (fxc_hbm, fxc),
            ]
        )
    ]
    for load in loads:
        load.start()

    barrier = pltpu.get_barrier_semaphore()

    def greet(step, _):
        pl.semaphore_signal(
            barrier, inc=1, device_id={"slab": lax.rem(me + step, slabs)}, device_id_type=MESH
        )
        return 0

    lax.fori_loop(1, slabs, greet, 0)
    pl.semaphore_signal(barrier, inc=1, device_id={"pool": partner}, device_id_type=MESH)

    loads[0].wait()

    def pick(slot, _):
        other[slot] = drho[owner_ref[partner * owned + slot]]
        return 0

    lax.fori_loop(0, owned, pick, 0)
    pl.semaphore_wait(barrier, slabs)

    def to_partner(slot):
        return pltpu.make_async_remote_copy(
            src_ref=other.at[slot],
            dst_ref=given.at[slot],
            send_sem=send_sem.at[0],
            recv_sem=other_sem.at[slot],
            device_id={"pool": partner},
            device_id_type=MESH,
        )

    def hand_over(slot, _):
        to_partner(slot).start()
        return 0

    lax.fori_loop(0, owned, hand_over, 0)

    def scatter(source, target, slot, arrived, left):
        def send(step, _):
            to = lax.rem(me + step, slabs)
            pltpu.make_async_remote_copy(
                src_ref=source.at[slot, to],
                dst_ref=target.at[slot, me],
                send_sem=left,
                recv_sem=arrived.at[slot],
                device_id={"slab": to},
                device_id_type=MESH,
            ).start()
            return 0

        lax.fori_loop(1, slabs, send, 0)
        target[slot, me] = source[slot, me]

    def await_all(target, slot, arrived):
        block = target.at[slot, pl.ds(0, slabs - 1)]
        pltpu.make_async_copy(block, block, arrived.at[slot]).wait()

    def await_sent(source, left):
        block = source.at[:, pl.ds(0, slabs - 1)]
        pltpu.make_async_copy(block, block, left).wait()

    loads[1].wait()
    loads[2].wait()

    def forward(slot, _):
        to_partner(slot).wait_recv()
        value = drho[owner_ref[pool * owned + slot]] + given[slot]
        density[slot] = value
        value = along_lanes(lanes, jnp.concatenate([value[:half], value[half:]], axis=1))
        value = from_left(spread, jnp.concatenate([value[:, :length], value[:, length:]], axis=0))
        sent[slot] = value.reshape(sent.shape[1:])
        scatter(sent, columns, slot, column_sem, send_sem.at[1])
        return 0

    lax.fori_loop(0, owned, forward, 0)

    for load in loads[3:]:
        load.wait()
    unit = (2.0 * math.pi / length) ** 2
    shape = (length, length)
    first = frequency(lax.broadcasted_iota(jnp.int32, shape, 0), length) ** 2
    last = frequency(lax.broadcasted_iota(jnp.int32, shape, 1), length) ** 2
    for part in range(width):
        middle = frequency(jnp.full(shape, me * width + part, jnp.int32), length) ** 2
        total = first + middle + last
        kept = mask[:, part, :].astype(jnp.float32)
        kernel[pl.ds(part * length, length)] = (
            4.0 * math.pi * kept / (unit * total + 0.25) * (1.0 / length**3)
        )

    def screen(slot, _):
        await_all(columns, slot, column_sem)
        value = from_left(gather, columns[slot].reshape(rows, length))
        factor = kernel[...]
        value = jnp.concatenate([value[:half] * factor, value[half:] * -factor], axis=0)
        back[slot] = from_left(spread, value).reshape(back.shape[1:])
        scatter(back, final, slot, final_sem, send_sem.at[2])
        return 0

    lax.fori_loop(0, owned, screen, 0)

    def outgoing(slot):
        place = out_hbm.at[pool * owned + slot]
        keep = pltpu.make_async_copy(result.at[slot], place, out_sem.at[0])
        give = pltpu.make_async_remote_copy(
            src_ref=result.at[slot],
            dst_ref=place,
            send_sem=out_sem.at[1],
            recv_sem=out_sem.at[2],
            device_id={"pool": partner},
            device_id_type=MESH,
        )
        return keep, give

    def inverse(slot, _):
        await_all(final, slot, final_sem)
        value = from_left(gather, final[slot].reshape(rows, length))
        value = along_lanes(lanes, jnp.concatenate([value[:half], value[half:]], axis=1))
        local = fxc[...]
        result[slot, pl.ds(0, half)] = value[:, :length] + local * density[slot, pl.ds(0, half)]
        result[slot, pl.ds(half, half)] = local * density[slot, pl.ds(half, half)] - value[:, length:]
        keep, give = outgoing(slot)
        keep.start()
        give.start()
        return 0

    lax.fori_loop(0, owned, inverse, 0)

    pltpu.make_async_copy(other, other, send_sem.at[0]).wait()
    await_sent(sent, send_sem.at[1])
    await_sent(back, send_sem.at[2])
    for n in range(3):
        pltpu.make_async_copy(result, result, out_sem.at[n]).wait()


def per_device(slabs, pools, drho_part, fxc, cutoff_mask, owner_table):
    _, slots, parts, planes, length, _ = drho_part.shape
    rows = parts * planes * length
    owned = slots // pools
    tables = dft_tables(length, planes)
    tile = parts * planes * planes
    field = (owned, rows, length)
    cut = (owned, slabs, tile, length)
    bf16, f32 = jnp.bfloat16, jnp.float32
    anywhere = pl.BlockSpec(memory_space=pl.ANY)
    out = pl.pallas_call(
        functools.partial(body, slabs, pools),
        out_shape=jax.ShapeDtypeStruct((slots, rows, length), f32),
        in_specs=[pl.BlockSpec(memory_space=pltpu.SMEM)] + [anywhere] * 6,
        out_specs=anywhere,
        scratch_shapes=[
            pltpu.VMEM((slots, rows, length), f32),
            pltpu.VMEM((planes * length, length), f32),
            pltpu.VMEM(cutoff_mask.shape, jnp.int32),
            *[pltpu.VMEM(table.shape, bf16) for table in tables],
            pltpu.VMEM((planes * length, length), f32),
            *[pltpu.VMEM(field, f32)] * 3,
            *[pltpu.VMEM(cut, f32)] * 4,
            pltpu.VMEM(field, f32),
            pltpu.SemaphoreType.DMA((6,)),
            pltpu.SemaphoreType.DMA((owned,)),
            pltpu.SemaphoreType.DMA((3,)),
            pltpu.SemaphoreType.DMA((owned,)),
            pltpu.SemaphoreType.DMA((owned,)),
            pltpu.SemaphoreType.DMA((3,)),
        ],
        compiler_params=pltpu.CompilerParams(
            collective_id=0, has_side_effects=True, vmem_limit_bytes=44 * 2**20
        ),
        name="response",
    )(
        owner_table,
        drho_part.reshape(slots, rows, length),
        fxc.reshape(planes * length, length),
        cutoff_mask,
        *[jnp.asarray(table) for table in tables],
    )
    return out.reshape(slots, parts, planes, length, length)


def solution(mesh):
    placed = (
        P("pool", "group", None, "slab", None, None),
        P("slab", None, None),
        P(None, "slab", None),
        P("group"),
    )
    return jax.shard_map(
        functools.partial(per_device, mesh.shape["slab"], mesh.shape["pool"]),
        mesh=mesh,
        in_specs=placed,
        out_specs=P("group", None, "slab", None, None),
        check_vma=False,
    )
```

time: 346 us -> 224 us (0.65); the launches traced: 341 us -> 224 us
  Pallas kernels: 0 us -> 216 us
  blocking collectives: 132 us -> 0 us
  waiting for transfers between devices: 117 us -> 0 us
  matrix products: 30.6 us -> 0 us
  local copies, waits for them, and re-layouts: 28.6 us -> 7.88 us
  between operations: 13.9 us -> 0.02 us
  starting transfers between devices: 9.98 us -> 0 us
  other arithmetic: 9.35 us -> 0 us
    pallas_call x0 -> x1, Pallas kernels: none -> 216 us  [per_device(): pl.pallas_call(functools.partial(body, slabs, pools), out_shape=jax.Shape...]
    all_to_all x2 -> x0, blocking collectives: 132 us -> none  [the longest x1 104 us: potentials(): lax.all_to_all(columns, 'slab', split_axis=2, concat_axis=3, tiled=True)]
    all_to_all x1 -> x0, waiting for transfers between devices: 94.8 us -> none  [potentials(): lax.all_to_all(spectrum, 'slab', split_axis=3, concat_axis=2, tiled=True)]
    dot_general x24 -> x0, matrix products: 30.6 us -> none  [the longest x6 7.72 us: transform(): imag_sin = jnp.einsum(form, imag_part, sine, precision=highest)]
    all_gather x1 -> x0, waiting for transfers between devices: 22.1 us -> none  [per_device(): return lax.all_gather(result, 'pool', axis=0, tiled=True)]
    another operation x2 -> x0, local copies, waits for them, and re-layouts: 15 us -> none  [transform(): jnp.stack([real_cos - orient * imag_sin, imag_cos + orient * real_sin], a...]
    all_to_all x1 -> x0, starting transfers between devices: 9.92 us -> none  [potentials(): lax.all_to_all(spectrum, 'slab', split_axis=3, concat_axis=2, tiled=True)]
    unnamed x4 -> x13, local copies, waits for them, and re-layouts: 0.01 us -> 7.88 us
  transfers between devices with their start and end apart: 2 -> 0, of which waited for: 2 -> 0; matrix products, arithmetic and copies ran while one was open for 0% -> 0% of each run, Pallas kernels for 0% -> 0%
where the time goes in v1:
time: 224 us
  Pallas kernels  216 us (96%)
  local copies, waits for them, and re-layouts  7.88 us (4%)
    pallas_call x1, Pallas kernels, per_device(): pl.pallas_call(functools.partial(body, slabs, pools), out_shape=jax.Shape...  216 us
    unnamed x13, local copies, waits for them, and re-layouts  7.88 us

profile of v1, /device:TPU:33, one launch (start us, length us, event | category | flops | bytes accessed | tf_op | source)
XLA Modules:
  0.0 223.8 jit_solution(8694794056658214291)
XLA Ops:
  0.0 0.0 copy-start
  0.0 1.2 copy-done
  1.2 0.0 copy-start.1
  1.2 1.2 copy-done.1
  2.5 0.0 copy-start.2
  2.5 0.9 copy-done.2
  3.4 0.0 copy-start.3
  3.4 0.9 copy-done.3
  4.3 0.0 copy-start.4
  4.3 0.9 copy-done.4
  5.2 0.0 copy-start.5
  5.2 0.7 copy-done.5
  5.9 215.9 %response.1 = f32[16,512,128]{2,1,0:T(8,128)S(1)} custom-call(s32[16]{0:T(128)S(1)} %copy-done.5, f32[16,512,128]{2,1,0:T(8,128)} %bitcast.5, f32[256,128]{1,0:T(8,128)S(1)} %bitcast.4, s32[128,2,128]{2,1,0:T(2,128)S(1)} %copy-done.4, bf16[2,256,256]{2,1,0:T(8,128)(2,1)S(1)} %copy-done.2, bf16[2,512,512]{2,1,0:T(8,128)(2,1)S(1)} %copy-done.1, ...), custom_call_target="tpu_custom_call" | custom-call | tf_op jit(solution)/shard_map/response/pallas_call | solution.py:242
  221.8 2.0 copy.9
Async XLA Ops:
  0.0 1.2 copy-start
  1.2 1.2 copy-start.1
  2.5 0.9 copy-start.2
  3.4 0.9 copy-start.3
  4.3 0.9 copy-start.4
  5.2 0.7 copy-start.5

commit v2 on v1

--- a/solution.py
+++ b/solution.py
@@ -67,8 +67,8 @@
 
 
 def body(
-    slabs, pools, owner_ref, drho_hbm, fxc_hbm, mask_hbm, lanes_hbm, spread_hbm, gather_hbm, out_hbm,
-    drho, fxc, mask, lanes, spread, gather, kernel, other, given, density, sent, columns, back, final, result,
+    slabs, pools, owner_hbm, drho_hbm, fxc_hbm, mask_hbm, lanes_hbm, spread_hbm, gather_hbm, out_hbm,
+    owner_ref, drho, fxc, mask, lanes, spread, gather, kernel, other, given, density, sent, columns, back, final, result,
     load_sem, other_sem, send_sem, column_sem, final_sem, out_sem,
 ):
     me = lax.axis_index("slab")
@@ -83,6 +83,7 @@
         pltpu.make_async_copy(source, target, load_sem.at[n])
         for n, (source, target) in enumerate(
             [
+                (owner_hbm, owner_ref),
                 (drho_hbm, drho),
                 (lanes_hbm, lanes),
                 (spread_hbm, spread),
@@ -107,6 +108,7 @@
     pl.semaphore_signal(barrier, inc=1, device_id={"pool": partner}, device_id_type=MESH)
 
     loads[0].wait()
+    loads[1].wait()
 
     def pick(slot, _):
         other[slot] = drho[owner_ref[partner * owned + slot]]
@@ -155,8 +157,8 @@
         block = source.at[:, pl.ds(0, slabs - 1)]
         pltpu.make_async_copy(block, block, left).wait()
 
-    loads[1].wait()
     loads[2].wait()
+    loads[3].wait()
 
     def forward(slot, _):
         to_partner(slot).wait_recv()
@@ -170,7 +172,7 @@
 
     lax.fori_loop(0, owned, forward, 0)
 
-    for load in loads[3:]:
+    for load in loads[4:]:
         load.wait()
     unit = (2.0 * math.pi / length) ** 2
     shape = (length, length)
@@ -239,12 +241,14 @@
     cut = (owned, slabs, tile, length)
     bf16, f32 = jnp.bfloat16, jnp.float32
     anywhere = pl.BlockSpec(memory_space=pl.ANY)
+    stays = pl.BlockSpec(memory_space=pltpu.HBM)
     out = pl.pallas_call(
         functools.partial(body, slabs, pools),
         out_shape=jax.ShapeDtypeStruct((slots, rows, length), f32),
-        in_specs=[pl.BlockSpec(memory_space=pltpu.SMEM)] + [anywhere] * 6,
+        in_specs=[stays] * 7,
         out_specs=anywhere,
         scratch_shapes=[
+            pltpu.SMEM(owner_table.shape, jnp.int32),
             pltpu.VMEM((slots, rows, length), f32),
             pltpu.VMEM((planes * length, length), f32),
             pltpu.VMEM(cutoff_mask.shape, jnp.int32),
@@ -253,7 +257,7 @@
             *[pltpu.VMEM(field, f32)] * 3,
             *[pltpu.VMEM(cut, f32)] * 4,
             pltpu.VMEM(field, f32),
-            pltpu.SemaphoreType.DMA((6,)),
+            pltpu.SemaphoreType.DMA((7,)),
             pltpu.SemaphoreType.DMA((owned,)),
             pltpu.SemaphoreType.DMA((3,)),
             pltpu.SemaphoreType.DMA((owned,)),
@@ -265,11 +269,16 @@
         ),
         name="response",
     )(
-        owner_table,
-        drho_part.reshape(slots, rows, length),
-        fxc.reshape(planes * length, length),
-        cutoff_mask,
-        *[jnp.asarray(table) for table in tables],
+        *[
+            pltpu.with_memory_space_constraint(value, pltpu.HBM)
+            for value in (
+                owner_table,
+                drho_part.reshape(slots, rows, length),
+                fxc.reshape(planes * length, length),
+                cutoff_mask,
+                *[jnp.asarray(table) for table in tables],
+            )
+        ]
     )
     return out.reshape(slots, parts, planes, length, length)
 

time: 224 us -> 217 us (0.969)
  local copies, waits for them, and re-layouts: 7.88 us -> 2.02 us
    unnamed x13 -> x1, local copies, waits for them, and re-layouts: 7.88 us -> 2.02 us
where the time goes in v2:
time: 217 us
  Pallas kernels  215 us (99%)
    pallas_call x1, Pallas kernels, per_device(): pl.pallas_call(functools.partial(body, slabs, pools), out_shape=jax.Shape...  215 us

profile of v2, /device:TPU:33, one launch (start us, length us, event | category | flops | bytes accessed | tf_op | source)
XLA Modules:
  0.0 216.8 jit_solution(12005955829128537878)
XLA Ops:
  0.0 214.8 %response.1 = f32[16,512,128]{2,1,0:T(8,128)S(1)} custom-call(s32[16]{0:T(128)} %owner_hbm.1, f32[16,512,128]{2,1,0:T(8,128)} %bitcast.4, f32[256,128]{1,0:T(8,128)} %bitcast.5, s32[128,2,128]{2,1,0:T(2,128)} %mask_hbm.1, bf16[2,256,256]{2,1,0:T(8,128)(2,1)} %constant.6.clone.lanes_hbm, bf16[2,512,512]{2,1,0:T(8,128)(2,1)} %constant.7.clone.spread_hbm, ...), custom_call_target="tpu_custom_call" | custom-call | tf_op jit(solution)/shard_map/response/pallas_call | solution.py:245
  214.8 2.0 copy.9

commit v3 on v2

--- a/solution.py
+++ b/solution.py
@@ -67,9 +67,9 @@
 
 
 def body(
-    slabs, pools, owner_hbm, drho_hbm, fxc_hbm, mask_hbm, lanes_hbm, spread_hbm, gather_hbm, out_hbm,
+    slabs, wide, pools, owner_hbm, drho_hbm, fxc_hbm, mask_hbm, lanes_hbm, spread_hbm, gather_hbm, out_hbm,
     owner_ref, drho, fxc, mask, lanes, spread, gather, kernel, other, given, density, sent, columns, back, final, result,
-    load_sem, other_sem, send_sem, column_sem, final_sem, out_sem,
+    load_sem, ready_sem, other_sem, send_sem, column_sem, final_sem, out_sem,
 ):
     me = lax.axis_index("slab")
     pool = lax.axis_index("pool")
@@ -97,15 +97,32 @@
         load.start()
 
     barrier = pltpu.get_barrier_semaphore()
-
-    def greet(step, _):
-        pl.semaphore_signal(
-            barrier, inc=1, device_id={"slab": lax.rem(me + step, slabs)}, device_id_type=MESH
-        )
-        return 0
-
-    lax.fori_loop(1, slabs, greet, 0)
+    turn = lax.rem(me + slabs - 1, slabs)
+    row = turn // wide
+    last = slabs // wide - 1
+
+    def at(position):
+        return lax.rem(position + 1, slabs)
+
+    def tell(semaphore, to):
+        pl.semaphore_signal(semaphore, inc=1, device_id={"slab": to}, device_id_type=MESH)
+
+    def greet(to, _):
+        @pl.when(to != turn)
+        def _():
+            tell(barrier, at(to))
+
+        return 0
+
+    lax.fori_loop(row * wide, slabs, greet, 0)
     pl.semaphore_signal(barrier, inc=1, device_id={"pool": partner}, device_id_type=MESH)
+    pl.semaphore_wait(barrier, (row + 1) * wide)
+
+    def announce(to, _):
+        tell(ready_sem.at[row], at(to))
+        return 0
+
+    lax.fori_loop(0, row * wide, announce, 0)
 
     loads[0].wait()
     loads[1].wait()
@@ -115,7 +132,6 @@
         return 0
 
     lax.fori_loop(0, owned, pick, 0)
-    pl.semaphore_wait(barrier, slabs)
 
     def to_partner(slot):
         return pltpu.make_async_remote_copy(
@@ -133,20 +149,32 @@
 
     lax.fori_loop(0, owned, hand_over, 0)
 
-    def scatter(source, target, slot, arrived, left):
-        def send(step, _):
-            to = lax.rem(me + step, slabs)
-            pltpu.make_async_remote_copy(
-                src_ref=source.at[slot, to],
-                dst_ref=target.at[slot, me],
-                send_sem=left,
-                recv_sem=arrived.at[slot],
-                device_id={"slab": to},
-                device_id_type=MESH,
-            ).start()
+    def send(source, target, slot, to, arrived, left):
+        pltpu.make_async_remote_copy(
+            src_ref=source.at[slot, to],
+            dst_ref=target.at[slot, me],
+            send_sem=left,
+            recv_sem=arrived.at[slot],
+            device_id={"slab": to},
+            device_id_type=MESH,
+        ).start()
+
+    def scatter(source, target, slot, among, arrived, left):
+        def one(step, _):
+            to = turn + step
+            send(source, target, slot, at(jnp.where(to < among, to, to - among)), arrived, left)
             return 0
 
-        lax.fori_loop(1, slabs, send, 0)
+        lax.fori_loop(1, among, one, 0)
+        target[slot, me] = source[slot, me]
+
+    def scatter_down(source, target, slot, arrived, left):
+        def one(step, _):
+            to = lax.rem(me + slabs - step, slabs)
+            send(source, target, slot, to, arrived, left)
+            return 0
+
+        lax.fori_loop(1, slabs, one, 0)
         target[slot, me] = source[slot, me]
 
     def await_all(target, slot, arrived):
@@ -160,27 +188,49 @@
     loads[2].wait()
     loads[3].wait()
 
-    def forward(slot, _):
+    def forward(slot):
         to_partner(slot).wait_recv()
         value = drho[owner_ref[pool * owned + slot]] + given[slot]
         density[slot] = value
         value = along_lanes(lanes, jnp.concatenate([value[:half], value[half:]], axis=1))
         value = from_left(spread, jnp.concatenate([value[:, :length], value[:, length:]], axis=0))
         sent[slot] = value.reshape(sent.shape[1:])
-        scatter(sent, columns, slot, column_sem, send_sem.at[1])
-        return 0
-
-    lax.fori_loop(0, owned, forward, 0)
+
+    early = 2
+    for slot in range(early):
+        forward(slot)
+        scatter(sent, columns, slot, (row + 1) * wide, column_sem, send_sem.at[1])
+    forward(early)
+
+    def later_row(to_row, _):
+        pl.semaphore_wait(ready_sem.at[to_row], wide)
+        for slot in range(early):
+            for step in range(wide):
+                send(sent, columns, slot, at(to_row * wide + step), column_sem, send_sem.at[1])
+        return 0
+
+    lax.fori_loop(row + 1, last + 1, later_row, 0)
+
+    def next_slot(slot, _):
+        scatter(sent, columns, slot, slabs, column_sem, send_sem.at[1])
+
+        @pl.when(slot + 1 < owned)
+        def _():
+            forward(slot + 1)
+
+        return 0
+
+    lax.fori_loop(early, owned, next_slot, 0)
 
     for load in loads[4:]:
         load.wait()
     unit = (2.0 * math.pi / length) ** 2
     shape = (length, length)
     first = frequency(lax.broadcasted_iota(jnp.int32, shape, 0), length) ** 2
-    last = frequency(lax.broadcasted_iota(jnp.int32, shape, 1), length) ** 2
+    third = frequency(lax.broadcasted_iota(jnp.int32, shape, 1), length) ** 2
     for part in range(width):
         middle = frequency(jnp.full(shape, me * width + part, jnp.int32), length) ** 2
-        total = first + middle + last
+        total = first + middle + third
         kept = mask[:, part, :].astype(jnp.float32)
         kernel[pl.ds(part * length, length)] = (
             4.0 * math.pi * kept / (unit * total + 0.25) * (1.0 / length**3)
@@ -192,7 +242,7 @@
         factor = kernel[...]
         value = jnp.concatenate([value[:half] * factor, value[half:] * -factor], axis=0)
         back[slot] = from_left(spread, value).reshape(back.shape[1:])
-        scatter(back, final, slot, final_sem, send_sem.at[2])
+        scatter_down(back, final, slot, final_sem, send_sem.at[2])
         return 0
 
     lax.fori_loop(0, owned, screen, 0)
@@ -235,6 +285,7 @@
     _, slots, parts, planes, length, _ = drho_part.shape
     rows = parts * planes * length
     owned = slots // pools
+    wide = next(n for n in range(math.isqrt(slabs) // 2, 0, -1) if slabs % n == 0)
     tables = dft_tables(length, planes)
     tile = parts * planes * planes
     field = (owned, rows, length)
@@ -243,7 +294,7 @@
     anywhere = pl.BlockSpec(memory_space=pl.ANY)
     stays = pl.BlockSpec(memory_space=pltpu.HBM)
     out = pl.pallas_call(
-        functools.partial(body, slabs, pools),
+        functools.partial(body, slabs, wide, pools),
         out_shape=jax.ShapeDtypeStruct((slots, rows, length), f32),
         in_specs=[stays] * 7,
         out_specs=anywhere,
@@ -258,6 +309,7 @@
             *[pltpu.VMEM(cut, f32)] * 4,
             pltpu.VMEM(field, f32),
             pltpu.SemaphoreType.DMA((7,)),
+            pltpu.SemaphoreType.REGULAR((slabs // wide,)),
             pltpu.SemaphoreType.DMA((owned,)),
             pltpu.SemaphoreType.DMA((3,)),
             pltpu.SemaphoreType.DMA((owned,)),

time: 217 us -> 215 us (level)
  no operation moved by 1% of the time
where the time goes in v3:
time: 215 us
  Pallas kernels  213 us (99%)
    pallas_call x1, Pallas kernels, per_device(): pl.pallas_call(functools.partial(body, slabs, wide, pools), out_shape=jax...  213 us

profile of v3, /device:TPU:33, one launch (start us, length us, event | category | flops | bytes accessed | tf_op | source)
XLA Modules:
  0.0 214.9 jit_solution(871227233100741753)
XLA Ops:
  0.0 212.9 %response.1 = f32[16,512,128]{2,1,0:T(8,128)S(1)} custom-call(s32[16]{0:T(128)} %owner_hbm.1, f32[16,512,128]{2,1,0:T(8,128)} %bitcast.4, f32[256,128]{1,0:T(8,128)} %bitcast.5, s32[128,2,128]{2,1,0:T(2,128)} %mask_hbm.1, bf16[2,256,256]{2,1,0:T(8,128)(2,1)} %constant.6.clone.lanes_hbm, bf16[2,512,512]{2,1,0:T(8,128)(2,1)} %constant.7.clone.spread_hbm, ...), custom_call_target="tpu_custom_call" | custom-call | tf_op jit(solution)/shard_map/response/pallas_call | solution.py:296
  212.9 2.0 copy.9

commit v4 on v3

--- a/solution.py
+++ b/solution.py
@@ -245,8 +245,6 @@
         scatter_down(back, final, slot, final_sem, send_sem.at[2])
         return 0
 
-    lax.fori_loop(0, owned, screen, 0)
-
     def outgoing(slot):
         place = out_hbm.at[pool * owned + slot]
         keep = pltpu.make_async_copy(result.at[slot], place, out_sem.at[0])
@@ -272,7 +270,15 @@
         give.start()
         return 0
 
-    lax.fori_loop(0, owned, inverse, 0)
+    lag = 2
+
+    def both(slot, _):
+        screen(slot, 0)
+        return inverse(slot - lag, 0)
+
+    lax.fori_loop(0, lag, screen, 0)
+    lax.fori_loop(lag, owned, both, 0)
+    lax.fori_loop(owned - lag, owned, inverse, 0)
 
     pltpu.make_async_copy(other, other, send_sem.at[0]).wait()
     await_sent(sent, send_sem.at[1])

time: 215 us -> 215 us (level)
  no operation moved by 1% of the time
where the time goes in v4:
time: 215 us
  Pallas kernels  213 us (99%)
    pallas_call x1, Pallas kernels, per_device(): pl.pallas_call(functools.partial(body, slabs, wide, pools), out_shape=jax...  213 us

profile of v4, /device:TPU:33, one launch (start us, length us, event | category | flops | bytes accessed | tf_op | source)
XLA Modules:
  0.0 214.9 jit_solution(16868344063175172593)
XLA Ops:
  0.0 212.9 %response.1 = f32[16,512,128]{2,1,0:T(8,128)S(1)} custom-call(s32[16]{0:T(128)} %owner_hbm.1, f32[16,512,128]{2,1,0:T(8,128)} %bitcast.4, f32[256,128]{1,0:T(8,128)} %bitcast.5, s32[128,2,128]{2,1,0:T(2,128)} %mask_hbm.1, bf16[2,256,256]{2,1,0:T(8,128)(2,1)} %constant.6.clone.lanes_hbm, bf16[2,512,512]{2,1,0:T(8,128)(2,1)} %constant.7.clone.spread_hbm, ...), custom_call_target="tpu_custom_call" | custom-call | tf_op jit(solution)/shard_map/response/pallas_call | solution.py:302
  212.9 2.0 copy.9
